TPU v7x, 32 devices: a whole 2x2x4 slice. The times are simulated.
32 devices in a mesh: band: 16 (over z, y, core), fft: 2 (over x).
Axes of the slice: x: 2, y: 2, z: 4, core: 2. Of those that a mesh axis runs over, the one named last changes fastest.
Arguments:
- coefficients: float32 [16, 2, 72, 5184], P('band', None, None, 'fft'), may hold values from -0.009765625 to 0.009765625
- col_index: int32 [5184], replicated, may hold values from 0 to 5183, each once
- occupation: int32 [16], P('band'), may hold values from 1 to 4
Outputs:
- density: float32 [288, 288, 288], P('band', 'fft')
Inputs may be any that keep to these rules, and one draw needn't show every extreme that they name: `col_index`: each number of the range appears once.
All inputs are finite; a program needn't handle non-finite values.
Results may differ from a plain program's by a relative error of at most 0.0003.
Values sent between devices are 32-bit elements; how exact they have to be, the bound alone decides.
A program may use at most 128 MiB of HBM per device.

v0:
```python
import math
import jax
import jax.numpy as jnp
from jax import lax
from jax.sharding import PartitionSpec as P

NC = 144
NF = 288
KZ = 72
NCOLS = 5184


def product(pattern, operand_a, operand_b):
    return jnp.einsum(pattern, operand_a, operand_b, precision=lax.Precision.HIGHEST)


def phase_tables(wave_count, offset, points):
    wave_index = jnp.arange(wave_count, dtype=jnp.int32) - offset
    grid_index = jnp.arange(points, dtype=jnp.int32)
    phases = jnp.mod(wave_index[:, None] * grid_index[None, :], points)
    angles = phases.astype(jnp.float32) * (2.0 * math.pi / points)
    return (jnp.cos(angles), jnp.sin(angles))


def interpolation_matrix(coarse_len, fine_len):
    fine_index = jnp.arange(fine_len, dtype=jnp.int32)
    coarse_index = jnp.arange(coarse_len, dtype=jnp.int32)
    wave_index = jnp.arange(1, coarse_len // 2, dtype=jnp.int32)
    offsets = fine_index[:, None] - 2 * coarse_index[None, :]
    phases = jnp.mod(offsets[:, :, None] * wave_index[None, None, :], fine_len)
    angles = phases.astype(jnp.float32) * (2.0 * math.pi / fine_len)
    return (1.0 + 2.0 * jnp.sum(jnp.cos(angles), axis=2)) / coarse_len


def rotate(pattern, real_part, imag_part, cos_table, sin_table):
    out_real = product(pattern, real_part, cos_table) - product(pattern, imag_part, sin_table)
    out_imag = product(pattern, real_part, sin_table) + product(pattern, imag_part, cos_table)
    return (out_real, out_imag)


def local(coefficients, col_index, occupation):
    band_here = coefficients.shape[0]
    col_count = coefficients.shape[3]
    band_total = band_here * lax.axis_size("band")
    radius = KZ // 2
    col_start = lax.axis_index("fft") * col_count
    local_cols = lax.dynamic_slice_in_dim(col_index, col_start, col_count)
    first_wave = local_cols // KZ - radius
    second_wave = local_cols % KZ - radius
    third_wave = jnp.arange(KZ, dtype=jnp.int32) - radius
    radial = (first_wave * first_wave + second_wave * second_wave)[None, :] + (
        third_wave * third_wave
    )[:, None]
    inside = (radial <= radius * radius).astype(jnp.float32)
    masked = coefficients * inside
    cos_table, sin_table = phase_tables(KZ, radius, NC)
    line_real, line_imag = rotate("bkc,kz->bzc", masked[:, 0], masked[:, 1], cos_table, sin_table)
    z_lines = jnp.stack([line_real, line_imag], axis=1)
    inverse = jnp.zeros((NCOLS,), jnp.int32).at[col_index].set(jnp.arange(NCOLS, dtype=jnp.int32))
    block_in = lax.all_to_all(z_lines, "fft", split_axis=2, concat_axis=3, tiled=True)
    box_grid = jnp.take(block_in, inverse, axis=3)
    box_grid = box_grid.reshape(block_in.shape[0], 2, block_in.shape[2], KZ, KZ)
    half_real, half_imag = rotate(
        "bzak,kr->bzar", box_grid[:, 0], box_grid[:, 1], cos_table, sin_table
    )
    full_real, full_imag = rotate("bzar,as->bzsr", half_real, half_imag, cos_table, sin_table)
    moduli = full_real * full_real + full_imag * full_imag
    weights = occupation.astype(jnp.float32) / band_total
    partial_value = product("b,bzxy->zxy", weights, moduli)
    interpolation = interpolation_matrix(NC, NF)
    row_share = NF // lax.axis_size("band")
    summed = lax.psum(partial_value, "band")
    own_rows = lax.dynamic_slice_in_dim(
        interpolation, lax.axis_index("band") * row_share, row_share, 0
    )
    reduced = product("zgb,fb->zgf", product("zab,ga->zgb", summed, own_rows), interpolation)
    return product(
        "rgf,hr->gfh",
        lax.all_to_all(reduced, "fft", split_axis=2, concat_axis=0, tiled=True),
        interpolation,
    )


def solution(mesh):
    return jax.shard_map(
        local,
        mesh=mesh,
        in_specs=(P("band", None, None, "fft"), P(), P("band")),
        out_specs=P("band", "fft", None),
        check_vma=False,
    )
```

profile of v0, /device:TPU:0, one launch (start us, length us, event | category | flops | bytes accessed | tf_op | source)
XLA Modules:
  0.0 451.8 jit_solution(9786847167849780601)
XLA Ops:
  19.3 4.2 all-to-all-start
  23.5 36.3 %scatter_custom_fusion = s32[5184]{0:T(1024)S(1)} fusion(s32[5184]{0:T(1024)S(1)} %compare_select_fusion.1, s32[5184]{0:T(1024)S(1)} %iota.59, s32[]{:T(128)} %constant.53.clone.1), kind=kCustom, calls=%fused_computation.112 | custom fusion | bytes 20740 | tf_op jit(solution)/shard_map/scatter | solution.py:59
  60.6 6.9 %copy.62 = f32[1,2,72,2,2592]{2,1,4,3,0:T(2,128)} copy(f32[1,2,72,2,2592]{4,1,2,3,0:T(2,128)S(1)} %bitcast.89) | data formatting | bytes 5971968 | tf_op jit(solution)/shard_map/all_to_all | solution.py:60
  67.5 19.1 %gather_fusion = f32[5184,2,72]{2,1,0:T(2,128)} fusion(f32[2,72,5184]{1,0,2:T(2,128)} %bitcast.87, s32[6144]{0:T(1024)S(1)} %pad_clamp_fusion), kind=kCustom, calls=%fused_computation | custom fusion | bytes 5992704 | tf_op jit(solution)/shard_map/jit(_take)/gather | solution.py:61
  86.6 8.5 %copy.63 = f32[1,2,72,72,72]{4,3,2,1,0:T(8,128)} copy(f32[1,2,72,72,72]{2,1,4,3,0:T(2,128)} %bitcast.88) | data formatting | bytes 5971968 | tf_op jit(solution)/shard_map/jit(_take)/gather | solution.py:61
  97.9 4.8 %fusion.10 = f32[72,72,144]{2,1,0:T(8,128)S(1)} fusion(f32[1,2,72,72,72]{4,3,2,1,0:T(8,128)S(1)} %broadcast_select_fusion, s32[72]{0:T(128)S(1)} %iota_add_fusion), kind=kOutput, calls=%fused_computation.22 | convolution fusion | flops 645065856 | bytes 5640704 | tf_op jit(solution)/shard_map/bzak,kr->bzar/dot_general | solution.py:14
  102.7 4.8 %fusion.13 = f32[72,72,144]{2,1,0:T(8,128)S(1)} fusion(f32[72,72,144]{2,1,0:T(8,128)S(1)} %fusion.10, f32[1,2,72,72,72]{4,3,2,1,0:T(8,128)S(1)} %broadcast_select_fusion, s32[72]{0:T(128)S(1)} %iota_add_fusion), kind=kOutput, calls=%fused_computation.25 | convolution fusion | flops 645812352 | bytes 10949120 | tf_op jit(solution)/shard_map/bzak,kr->bzar/dot_general | solution.py:14
  107.5 11.8 %fusion.26 = f32[144,72,144]{2,0,1:T(8,128)} fusion(f32[72,72,144]{2,1,0:T(8,128)S(1)} %fusion.13, s32[72]{0:T(128)S(1)} %iota_add_fusion), kind=kOutput, calls=%fused_computation.46 | convolution fusion | flops 1290038400 | bytes 8958240 | tf_op jit(solution)/shard_map/bzar,as->bzsr/dot_general | solution.py:14
  119.3 12.0 %fusion.34 = f32[144,72,144]{2,0,1:T(8,128)} fusion(f32[72,72,144]{2,1,0:T(8,128)S(1)} %fusion.13, s32[72]{0:T(128)S(1)} %iota_add_fusion), kind=kOutput, calls=%fused_computation.54 | convolution fusion | flops 1290038400 | bytes 8958240 | tf_op jit(solution)/shard_map/bzar,as->bzsr/dot_general | solution.py:14
  131.3 4.8 %fusion.9 = f32[72,72,144]{2,1,0:T(8,128)S(1)} fusion(f32[1,2,72,72,72]{4,3,2,1,0:T(8,128)S(1)} %broadcast_select_fusion, s32[72]{0:T(128)S(1)} %iota_add_fusion), kind=kOutput, calls=%fused_computation.21 | convolution fusion | flops 645065856 | bytes 5640704 | tf_op jit(solution)/shard_map/bzak,kr->bzar/dot_general | solution.py:14
  136.1 4.8 %fusion.14 = f32[72,72,144]{2,1,0:T(8,128)S(1)} fusion(f32[72,72,144]{2,1,0:T(8,128)S(1)} %fusion.9, f32[1,2,72,72,72]{4,3,2,1,0:T(8,128)S(1)} %broadcast_select_fusion, s32[72]{0:T(128)S(1)} %iota_add_fusion), kind=kOutput, calls=%fused_computation.26 | convolution fusion | flops 645812352 | bytes 10949120 | tf_op jit(solution)/shard_map/bzak,kr->bzar/dot_general | solution.py:14
  140.9 11.7 %fusion.28 = f32[144,72,144]{2,0,1:T(8,128)} fusion(f32[72,72,144]{2,1,0:T(8,128)S(1)} %fusion.14, s32[72]{0:T(128)S(1)} %iota_add_fusion), kind=kOutput, calls=%fused_computation.48 | convolution fusion | flops 1290038400 | bytes 8958240 | tf_op jit(solution)/shard_map/bzar,as->bzsr/dot_general | solution.py:14
  152.6 21.9 %multiply_bitcast_fusion = f32[72,144,144]{2,1,0:T(8,128)} fusion(f32[144,72,144]{2,0,1:T(8,128)} %fusion.26, f32[144,72,144]{2,0,1:T(8,128)} %fusion.34, f32[144,72,144]{2,0,1:T(8,128)} %fusion.28, f32[]{:T(128)} %bitcast.1, f32[72,72,144]{2,1,0:T(8,128)} %copy-done, s32[72]{0:T(128)S(1)} %iota_add_fusion), kind=kOutput, calls=%fused_computation.11 | convolution fusion | flops 1298996352 | bytes 26874148 | tf_op jit(solution)/shard_map/bzar,as->bzsr/dot_general | solution.py:14
  174.6 61.2 %fusion.3 = f32[288,144]{0,1:T(8,128)S(1)} fusion(s32[71]{0:T(128)S(1)} %iota_add_fusion.1, s32[288,144]{0,1:T(8,128)S(1)} %iota_subtract_fusion), kind=kLoop, calls=%fused_computation.6 | loop fusion | flops 29403648 | bytes 332060 | tf_op jit(solution)/shard_map/reduce_sum | solution.py:32
  235.9 144.0 %all-reduce.2.cloned.1.call-done = f32[72,144,144]{2,1,0:T(8,128)} async-done(((f32[72,144,144]{2,1,0:T(8,128)}), f32[72,144,144]{2,1,0:T(8,128)}) %all-reduce.2.cloned.1.call-update) | async-done | bytes 5971984 | tf_op jit(solution)/shard_map/psum | solution.py:72
  379.9 8.3 %convolution_bitcast_fusion = f32[72,18,144]{2,1,0:T(8,128)S(1)} fusion(f32[72,144,144]{2,1,0:T(8,128)} %all-reduce.2.cloned.1.call-done, f32[288,144]{0,1:T(8,128)S(1)} %add_multiply_fusion, s32[]{:T(128)S(6)} %select_n.74), kind=kOutput, calls=%fused_computation.27 | convolution fusion | flops 322486272 | bytes 6792196 | tf_op jit(solution)/shard_map/zab,ga->zgb/dot_general | solution.py:14
  388.2 3.8 fusion.15
  392.0 3.5 copy.54
  395.5 3.8 reshape.191
  399.2 22.0 %all_to_all.36 = f32[2,1,186624]{2,1,0:T(1,128)S(1)} all-to-all(f32[2,1,186624]{2,1,0:T(1,128)} %reshape.191), channel_id=1, replica_groups=mesh['band'=16,'fft'=2] {'fft'}, dimensions={0} | all-to-all | bytes 2985984 | tf_op jit(solution)/shard_map/all_to_all | solution.py:79
  421.8 6.2 %reduce = f32[2,186624]{1,0:T(2,128)} reduce(f32[2,1,186624]{2,1,0:T(1,128)S(1)} %all_to_all.36, f32[]{:T(128)} %broadcast.120), dimensions={1}, to_apply=%all_to_all.30.reduce_sub_computation | reduce | bytes 2985988 | tf_op jit(solution)/shard_map/all_to_all | solution.py:79
  428.0 4.1 reshape.192
  432.1 3.6 copy.72
  439.0 5.8 %fusion.20 = f32[18,144,288]{2,1,0:T(8,128)} fusion(f32[144,18,144]{0,2,1:T(8,128)S(1)} %all_to_all.33, f32[288,144]{0,1:T(8,128)S(1)} %copy-done.2), kind=kOutput, calls=%fused_computation.37 | convolution fusion | flops 1290069504 | bytes 4644864 | tf_op jit(solution)/shard_map/rgf,hr->gfh/dot_general | solution.py:14
  (35 shorter events, 19.7 us)
Async XLA Ops:
  16.0 7.5 %copy-start.3 = (s32[5184]{0:T(1024)S(1)}, s32[5184]{0:T(1024)}, u32[]{:S(2)}) copy-start(s32[5184]{0:T(1024)} %param.4) | copy-start | bytes 62212
  19.3 41.3 %all-to-all-start = ((f32[1,2,144,2592]{3,1,0,2:T(2,128)}), f32[1,2,144,2592]{3,1,0,2:T(2,128)S(1)}, u32[]{:S(2)}, u32[]{:S(2)}) async-start(f32[1,2,144,2592]{3,1,0,2:T(2,128)} %copy.44), calls=%async_computation | async-start | bytes 6193152 | tf_op jit(solution)/shard_map/all_to_all | solution.py:60
  23.5 356.4 %all-reduce.2.cloned.1.call-start = ((), (), s32[]{:S(2)}) async-start(), calls=%async_computation.2 | async-start | bytes 21233664 | tf_op jit(solution)/shard_map/psum | solution.py:72
  140.9 11.7 %copy-start = (f32[72,72,144]{2,1,0:T(8,128)}, f32[72,72,144]{2,1,0:T(8,128)S(1)}, u32[]{:S(2)}) copy-start(f32[72,72,144]{2,1,0:T(8,128)S(1)} %fusion.14) | copy-start | bytes 8957956
  235.8 152.3 %copy-start.1 = (f32[288,144]{0,1:T(8,128)}, f32[288,144]{0,1:T(8,128)S(1)}, u32[]{:S(2)}) copy-start(f32[288,144]{0,1:T(8,128)S(1)} %fusion.3) | copy-start | bytes 497668
  435.7 3.3 copy-start.2
Sparse Core Ops, SparseCore 0:
  174.6 205.2 all-reduce.1
where the time goes:
time: 460 us; the launch traced here: 452 us
  waiting for transfers between devices  144 us (31%)
  matrix products  101 us (22%)
  local copies, waits for them, and re-layouts  92.8 us (20%)
  other arithmetic  73.2 us (16%)
  blocking collectives  22 us (5%)
  between operations  14.5 us (3%)
    psum x1, waiting for transfers between devices, local(): summed = lax.psum(partial_value, 'band')  144 us
    dot_general x15, matrix products, product(): jnp.einsum(pattern, operand_a, operand_b, precision=lax.Precision.HIGHEST)  101 us
    reduce_sum x1, other arithmetic, interpolation_matrix(): return (1.0 + 2.0 * jnp.sum(jnp.cos(angles), axis=2)) / coarse_len  61.2 us
    scatter x1, local copies, waits for them, and re-layouts, local(): jnp.zeros((NCOLS,), jnp.int32).at[col_index]  36.3 us
    gather x2, local copies, waits for them, and re-layouts, local(): box_grid = jnp.take(block_in, inverse, axis=3)  27.5 us
    all_to_all x1, blocking collectives, local(): lax.all_to_all(reduced, 'fft', split_axis=2, concat_axis=0, tiled=True)  22 us
  transfers between devices with their start and end apart: 2, of which 1 were waited for; matrix products, arithmetic and copies ran while one was open for 22% of the time, Pallas kernels for 0%

commit v1 on v0

--- a/solution.py
+++ b/solution.py
@@ -8,6 +8,13 @@
 NF = 288
 KZ = 72
 NCOLS = 5184
+
+
+def swap_blocks(x, axis, split, join):
+    size = lax.axis_size(axis)
+    pieces = jnp.stack(jnp.split(x, size, axis=split), axis=0)
+    pieces = lax.all_to_all(pieces, axis, split_axis=0, concat_axis=0)
+    return jnp.concatenate(pieces, axis=join)
 
 
 def product(pattern, operand_a, operand_b):
@@ -74,11 +81,7 @@
         interpolation, lax.axis_index("band") * row_share, row_share, 0
     )
     reduced = product("zgb,fb->zgf", product("zab,ga->zgb", summed, own_rows), interpolation)
-    return product(
-        "rgf,hr->gfh",
-        lax.all_to_all(reduced, "fft", split_axis=2, concat_axis=0, tiled=True),
-        interpolation,
-    )
+    return product("rgf,hr->gfh", swap_blocks(reduced, "fft", 2, 0), interpolation)
 
 
 def solution(mesh):

time: 460 us -> 444 us (0.965)
  local copies, waits for them, and re-layouts: 92.8 us -> 64.3 us
  blocking collectives: 22 us -> 33.4 us
  waiting for transfers between devices: 144 us -> 152 us
  other arithmetic: 73.2 us -> 67.2 us
    all_to_all x1, blocking collectives: 22 us -> 33.4 us  [swap_blocks(): pieces = lax.all_to_all(pieces, axis, split_axis=0, concat_axis=0)]
    scatter x1, local copies, waits for them, and re-layouts: 36.3 us -> 25.7 us  [local(): jnp.zeros((NCOLS,), jnp.int32).at[col_index]]
    all_to_all x1, waiting for transfers between devices: 0.01 us -> 10.1 us  [local(): lax.all_to_all(z_lines, 'fft', split_axis=2, concat_axis=3, tiled=True)]
    unnamed x10 -> x4, local copies, waits for them, and re-layouts: 7.84 us -> 0.01 us
    all_to_all x3 -> x1, local copies, waits for them, and re-layouts: 7.45 us -> 0.34 us  [swap_blocks(): pieces = lax.all_to_all(pieces, axis, split_axis=0, concat_axis=0)]
    all_to_all x1 -> x0, other arithmetic: 6.22 us -> none  [local(): lax.all_to_all(reduced, 'fft', split_axis=2, concat_axis=0, tiled=True)]
  transfers between devices with their start and end apart: 2 -> 2, of which waited for: 1 -> 2; matrix products, arithmetic and copies ran while one was open for 22% -> 20% of each run, Pallas kernels for 0% -> 0%
where the time goes in v1:
time: 444 us; the launch traced here: 437 us
  waiting for transfers between devices  152 us (34%)
  matrix products  101 us (23%)
  other arithmetic  67.2 us (15%)
  local copies, waits for them, and re-layouts  64.3 us (14%)
  blocking collectives  33.4 us (8%)
  between operations  14.5 us (3%)
    psum x1, waiting for transfers between devices, local(): summed = lax.psum(partial_value, 'band')  142 us
    dot_general x15, matrix products, product(): jnp.einsum(pattern, operand_a, operand_b, precision=lax.Precision.HIGHEST)  101 us
    reduce_sum x1, other arithmetic, interpolation_matrix(): return (1.0 + 2.0 * jnp.sum(jnp.cos(angles), axis=2)) / coarse_len  61.2 us
    all_to_all x1, blocking collectives, swap_blocks(): pieces = lax.all_to_all(pieces, axis, split_axis=0, concat_axis=0)  33.4 us
    gather x2, local copies, waits for them, and re-layouts, local(): box_grid = jnp.take(block_in, inverse, axis=3)  27.5 us
    scatter x1, local copies, waits for them, and re-layouts, local(): jnp.zeros((NCOLS,), jnp.int32).at[col_index]  25.7 us
    all_to_all x1, waiting for transfers between devices, local(): lax.all_to_all(z_lines, 'fft', split_axis=2, concat_axis=3, tiled=True)  10.1 us
  transfers between devices with their start and end apart: 2, of which 2 were waited for; matrix products, arithmetic and copies ran while one was open for 20% of the time, Pallas kernels for 0%

profile of v1, /device:TPU:0, one launch (start us, length us, event | category | flops | bytes accessed | tf_op | source)
XLA Modules:
  0.0 436.8 jit_solution(9423977052583883542)
XLA Ops:
  12.4 1.7 fusion.8
  14.1 1.7 fusion.7
  16.1 3.2 copy.44
  19.3 4.2 all-to-all-start
  23.5 25.7 %scatter_custom_fusion = s32[5184]{0:T(1024)S(1)} fusion(s32[5184]{0:T(1024)S(1)} %compare_select_fusion.1, s32[5184]{0:T(1024)S(1)} %iota.59, s32[]{:T(128)} %constant.53.clone.1), kind=kCustom, calls=%fused_computation.114 | custom fusion | bytes 20740 | tf_op jit(solution)/shard_map/scatter | solution.py:66
  50.1 10.1 %all-to-all-done = f32[1,2,144,2592]{3,1,0,2:T(2,128)S(1)} async-done(((f32[1,2,144,2592]{3,1,0,2:T(2,128)}), f32[1,2,144,2592]{3,1,0,2:T(2,128)S(1)}, u32[]{:S(2)}, u32[]{:S(2)}) %all-to-all-start) | async-done | bytes 2986016 | tf_op jit(solution)/shard_map/all_to_all | solution.py:67
  60.3 6.9 %copy.63 = f32[1,2,72,2,2592]{2,1,4,3,0:T(2,128)} copy(f32[1,2,72,2,2592]{4,1,2,3,0:T(2,128)S(1)} %bitcast.84) | data formatting | bytes 5971968 | tf_op jit(solution)/shard_map/all_to_all | solution.py:67
  67.2 19.1 %gather_fusion = f32[5184,2,72]{2,1,0:T(2,128)} fusion(f32[2,72,5184]{1,0,2:T(2,128)} %bitcast.82, s32[6144]{0:T(1024)S(1)} %pad_clamp_fusion), kind=kCustom, calls=%fused_computation | custom fusion | bytes 5992704 | tf_op jit(solution)/shard_map/jit(_take)/gather | solution.py:68
  86.2 8.5 %copy.64 = f32[1,2,72,72,72]{4,3,2,1,0:T(8,128)} copy(f32[1,2,72,72,72]{2,1,4,3,0:T(2,128)} %bitcast.83) | data formatting | bytes 5971968 | tf_op jit(solution)/shard_map/jit(_take)/gather | solution.py:68
  94.7 2.9 broadcast_select_fusion
  97.6 4.8 %fusion.10 = f32[72,72,144]{2,1,0:T(8,128)S(1)} fusion(f32[1,2,72,72,72]{4,3,2,1,0:T(8,128)S(1)} %broadcast_select_fusion, s32[72]{0:T(128)S(1)} %iota_add_fusion), kind=kOutput, calls=%fused_computation.22 | convolution fusion | flops 645065856 | bytes 5640704 | tf_op jit(solution)/shard_map/bzak,kr->bzar/dot_general | solution.py:21
  102.4 4.8 %fusion.13 = f32[72,72,144]{2,1,0:T(8,128)S(1)} fusion(f32[72,72,144]{2,1,0:T(8,128)S(1)} %fusion.10, f32[1,2,72,72,72]{4,3,2,1,0:T(8,128)S(1)} %broadcast_select_fusion, s32[72]{0:T(128)S(1)} %iota_add_fusion), kind=kOutput, calls=%fused_computation.25 | convolution fusion | flops 645812352 | bytes 10949120 | tf_op jit(solution)/shard_map/bzak,kr->bzar/dot_general | solution.py:21
  107.2 11.8 %fusion.26 = f32[144,72,144]{2,0,1:T(8,128)} fusion(f32[72,72,144]{2,1,0:T(8,128)S(1)} %fusion.13, s32[72]{0:T(128)S(1)} %iota_add_fusion), kind=kOutput, calls=%fused_computation.48 | convolution fusion | flops 1290038400 | bytes 8958240 | tf_op jit(solution)/shard_map/bzar,as->bzsr/dot_general | solution.py:21
  118.9 11.8 %fusion.34 = f32[144,72,144]{2,0,1:T(8,128)} fusion(f32[72,72,144]{2,1,0:T(8,128)S(1)} %fusion.13, s32[72]{0:T(128)S(1)} %iota_add_fusion), kind=kOutput, calls=%fused_computation.56 | convolution fusion | flops 1290038400 | bytes 8958240 | tf_op jit(solution)/shard_map/bzar,as->bzsr/dot_general | solution.py:21
  130.8 4.8 %fusion.9 = f32[72,72,144]{2,1,0:T(8,128)S(1)} fusion(f32[1,2,72,72,72]{4,3,2,1,0:T(8,128)S(1)} %broadcast_select_fusion, s32[72]{0:T(128)S(1)} %iota_add_fusion), kind=kOutput, calls=%fused_computation.21 | convolution fusion | flops 645065856 | bytes 5640704 | tf_op jit(solution)/shard_map/bzak,kr->bzar/dot_general | solution.py:21
  135.5 4.8 %fusion.14 = f32[72,72,144]{2,1,0:T(8,128)S(1)} fusion(f32[72,72,144]{2,1,0:T(8,128)S(1)} %fusion.9, f32[1,2,72,72,72]{4,3,2,1,0:T(8,128)S(1)} %broadcast_select_fusion, s32[72]{0:T(128)S(1)} %iota_add_fusion), kind=kOutput, calls=%fused_computation.26 | convolution fusion | flops 645812352 | bytes 10949120 | tf_op jit(solution)/shard_map/bzak,kr->bzar/dot_general | solution.py:21
  140.3 11.9 %fusion.28 = f32[144,72,144]{2,0,1:T(8,128)} fusion(f32[72,72,144]{2,1,0:T(8,128)S(1)} %fusion.14, s32[72]{0:T(128)S(1)} %iota_add_fusion), kind=kOutput, calls=%fused_computation.50 | convolution fusion | flops 1290038400 | bytes 8958240 | tf_op jit(solution)/shard_map/bzar,as->bzsr/dot_general | solution.py:21
  152.3 21.6 %multiply_bitcast_fusion = f32[72,144,144]{2,1,0:T(8,128)} fusion(f32[144,72,144]{2,0,1:T(8,128)} %fusion.26, f32[144,72,144]{2,0,1:T(8,128)} %fusion.34, f32[144,72,144]{2,0,1:T(8,128)} %fusion.28, f32[]{:T(128)} %bitcast.1, f32[72,72,144]{2,1,0:T(8,128)} %copy-done, s32[72]{0:T(128)S(1)} %iota_add_fusion), kind=kOutput, calls=%fused_computation.11 | convolution fusion | flops 1298996352 | bytes 26874148 | tf_op jit(solution)/shard_map/bzar,as->bzsr/dot_general | solution.py:21
  174.0 61.2 %fusion.3 = f32[288,144]{0,1:T(8,128)S(1)} fusion(s32[71]{0:T(128)S(1)} %iota_add_fusion.1, s32[288,144]{0,1:T(8,128)S(1)} %iota_subtract_fusion), kind=kLoop, calls=%fused_computation.6 | loop fusion | flops 29403648 | bytes 332060 | tf_op jit(solution)/shard_map/reduce_sum | solution.py:39
  235.2 141.7 %all-reduce.2.cloned.1.call-done = f32[72,144,144]{2,1,0:T(8,128)} async-done(((f32[72,144,144]{2,1,0:T(8,128)}), f32[72,144,144]{2,1,0:T(8,128)}) %all-reduce.2.cloned.1.call-update) | async-done | bytes 5971984 | tf_op jit(solution)/shard_map/psum | solution.py:79
  376.9 8.1 %convolution_bitcast_fusion = f32[72,18,144]{2,1,0:T(8,128)S(1)} fusion(f32[72,144,144]{2,1,0:T(8,128)} %all-reduce.2.cloned.1.call-done, f32[288,144]{0,1:T(8,128)S(1)} %add_multiply_fusion, s32[]{:T(128)S(6)} %select_n.74), kind=kOutput, calls=%fused_computation.27 | convolution fusion | flops 322486272 | bytes 6792196 | tf_op jit(solution)/shard_map/zab,ga->zgb/dot_general | solution.py:21
  385.0 2.6 fusion.15
  388.2 33.4 %all_to_all.23 = f32[2,72,18,144]{3,1,2,0:T(8,128)S(1)} all-to-all(f32[2,72,18,144]{3,1,2,0:T(8,128)S(1)} %pad_maximum_fusion.1), channel_id=1, replica_groups=mesh['band'=16,'fft'=2] {'fft'}, dimensions={0} | all-to-all | bytes 2985984 | tf_op jit(solution)/shard_map/all_to_all | solution.py:16
  422.0 7.7 %fusion.20 = f32[18,144,288]{2,1,0:T(8,128)} fusion(f32[144,18,144]{2,0,1:T(8,128)S(1)} %bitcast.85, f32[288,144]{0,1:T(8,128)S(1)} %fusion.3), kind=kOutput, calls=%fused_computation.39 | convolution fusion | flops 1290069504 | bytes 4644864 | tf_op jit(solution)/shard_map/rgf,hr->gfh/dot_general | solution.py:21
  (27 shorter events, 7.3 us)
Async XLA Ops:
  16.0 7.5 %copy-start.1 = (s32[5184]{0:T(1024)S(1)}, s32[5184]{0:T(1024)}, u32[]{:S(2)}) copy-start(s32[5184]{0:T(1024)} %param.4) | copy-start | bytes 62212
  19.3 41.0 %all-to-all-start = ((f32[1,2,144,2592]{3,1,0,2:T(2,128)}), f32[1,2,144,2592]{3,1,0,2:T(2,128)S(1)}, u32[]{:S(2)}, u32[]{:S(2)}) async-start(f32[1,2,144,2592]{3,1,0,2:T(2,128)} %copy.44), calls=%async_computation | async-start | bytes 6193152 | tf_op jit(solution)/shard_map/all_to_all | solution.py:67
  23.5 353.4 %all-reduce.2.cloned.1.call-start = ((), (), s32[]{:S(2)}) async-start(), calls=%async_computation.2 | async-start | bytes 21233664 | tf_op jit(solution)/shard_map/psum | solution.py:79
  140.3 11.9 %copy-start = (f32[72,72,144]{2,1,0:T(8,128)}, f32[72,72,144]{2,1,0:T(8,128)S(1)}, u32[]{:S(2)}) copy-start(f32[72,72,144]{2,1,0:T(8,128)S(1)} %fusion.14) | copy-start | bytes 8957956
Sparse Core Ops, SparseCore 0:
  174.0 202.8 all-reduce.1
